TPU v7x, 8 devices: a whole 2x2x1 slice. The times are simulated.
8 devices in a mesh: stage: 4 (over z, y, x), data: 2 (over core).
Axes of the slice: x: 2, y: 2, z: 1, core: 2. Of those that a mesh axis runs over, the one named last changes fastest.
Arguments:
- x_in: bfloat16 [4, 8192, 1024], P(None, 'data')
- targets: bfloat16 [4, 8192, 1024], P(None, 'data')
- w_work: bfloat16 [4, 1, 8388608], P('stage')
- w_master: float32 [4, 1, 8388608], P('stage', None, 'data')
- m_prior: float32 [4, 1, 8388608], P('stage', None, 'data')
- v_prior: float32 [4, 1, 8388608], P('stage', None, 'data')
- clip_tau: float32 [], replicated
Outputs:
- output 1: float32 [], replicated
- output 2: bfloat16 [4, 1, 8388608], P('stage')
- output 3: float32 [4, 1, 8388608], P('stage', None, 'data')
- output 4: float32 [4, 1, 8388608], P('stage', None, 'data')
- output 5: float32 [4, 1, 8388608], P('stage', None, 'data')
All inputs are finite; a program needn't handle non-finite values.
Results may differ from a plain program's by a relative error of at most 0.001.
Values are sent between devices in bfloat16 or wider.
A program may use at most 1 GiB of HBM per device.

v0:
```python
import math
import jax
import jax.numpy as jnp
from jax import lax
from jax.sharding import PartitionSpec as P

ADAM_BETA1 = 0.9
ADAM_BETA2 = 0.95
ADAM_EPS = 1e-8
WEIGHT_DECAY = 0.1
ADAM_STEP = 10
LR_BASE = 0.05


def gelu_tanh(z_val):
    return jax.nn.gelu(z_val, approximate=True)


def split_layer(w_flat, d_model):
    half_len = 4 * d_model * d_model
    return w_flat[:half_len].reshape(d_model, 4 * d_model), w_flat[half_len:].reshape(4 * d_model, d_model)


def stage_forward(hidden, w_in_list, w_out_list):
    saved_in = []
    saved_pre = []
    for w_in, w_out in zip(w_in_list, w_out_list):
        pre_act = jnp.dot(hidden, w_in, preferred_element_type=jnp.float32).astype(jnp.bfloat16)
        act_bf = gelu_tanh(pre_act.astype(jnp.float32)).astype(jnp.bfloat16)
        saved_in.append(hidden)
        saved_pre.append(pre_act)
        hidden = (hidden.astype(jnp.float32) + jnp.dot(act_bf, w_out, preferred_element_type=jnp.float32)).astype(jnp.bfloat16)
    return hidden, jnp.stack(saved_in), jnp.stack(saved_pre)


def stage_backward(grad_h, saved_in, saved_pre, w_in_list, w_out_list, acc_in, acc_out):
    acc_in = list(acc_in)
    acc_out = list(acc_out)
    for layer_idx in reversed(range(len(w_in_list))):
        act_f, gelu_pull = jax.vjp(gelu_tanh, saved_pre[layer_idx].astype(jnp.float32))
        act_bf = act_f.astype(jnp.bfloat16)
        grad_act = jnp.einsum('nk,fk->nf', grad_h, w_out_list[layer_idx], preferred_element_type=jnp.float32)
        grad_pre = gelu_pull(grad_act)[0].astype(jnp.bfloat16)
        acc_out[layer_idx] = acc_out[layer_idx] + jnp.einsum('nf,nk->fk', act_bf, grad_h, preferred_element_type=jnp.float32)
        acc_in[layer_idx] = acc_in[layer_idx] + jnp.einsum('nk,nf->kf', saved_in[layer_idx], grad_pre, preferred_element_type=jnp.float32)
        grad_h = (grad_h.astype(jnp.float32) + jnp.einsum('nf,kf->nk', grad_pre, w_in_list[layer_idx], preferred_element_type=jnp.float32)).astype(jnp.bfloat16)
    return grad_h, acc_in, acc_out


def run_stages(x_in, targets, w_work, stages, data_size):
    micro_n, tok_rows, d_model = x_in.shape
    layers = w_work.shape[1]
    token_count = micro_n * tok_rows * data_size
    stage_idx = lax.axis_index('stage')
    is_first = stage_idx == 0
    is_last = stage_idx == stages - 1
    w_in_list = []
    w_out_list = []
    for layer_idx in range(layers):
        w_in, w_out = split_layer(w_work[0, layer_idx], d_model)
        w_in_list.append(w_in)
        w_out_list.append(w_out)
    stash_slots = min(micro_n, 2 * stages - 1)
    tick_count = micro_n + 2 * stages - 2
    fwd_pairs = [(src, src + 1) for src in range(stages - 1)]
    bwd_pairs = [(src + 1, src) for src in range(stages - 1)]

    def tick_body(tick_idx, loop_state):
        recv_act, recv_grad, stash_in, stash_pre, acc_in, acc_out, loss_acc = loop_state
        fwd_id = tick_idx - stage_idx
        fwd_ok = (fwd_id >= 0) & (fwd_id < micro_n)
        fwd_safe = jnp.clip(fwd_id, 0, micro_n - 1)
        first_rows = lax.dynamic_index_in_dim(x_in, fwd_safe, 0, keepdims=False)
        act_in = jnp.where(is_first, first_rows, recv_act)

        def run_fwd(hidden):
            return stage_forward(hidden, w_in_list, w_out_list)

        def skip_fwd(hidden):
            return hidden, jnp.zeros((layers, tok_rows, d_model), jnp.bfloat16), jnp.zeros((layers, tok_rows, 4 * d_model), jnp.bfloat16)

        act_out, new_in, new_pre = lax.cond(fwd_ok, run_fwd, skip_fwd, act_in)
        write_slot = jnp.where(fwd_ok, fwd_safe % stash_slots, stash_slots)
        stash_in = lax.dynamic_update_index_in_dim(stash_in, new_in, write_slot, 0)
        stash_pre = lax.dynamic_update_index_in_dim(stash_pre, new_pre, write_slot, 0)
        target_rows = lax.dynamic_index_in_dim(targets, fwd_safe, 0, keepdims=False)
        residual = act_out.astype(jnp.float32) - target_rows.astype(jnp.float32)
        loss_acc = loss_acc + jnp.where(fwd_ok & is_last, 0.5 * jnp.sum(residual * residual), 0.0)
        top_grad = (residual / token_count).astype(jnp.bfloat16)
        bwd_id = tick_idx - (2 * stages - 2 - stage_idx)
        bwd_ok = (bwd_id >= 0) & (bwd_id < micro_n)
        read_slot = jnp.clip(bwd_id, 0, micro_n - 1) % stash_slots
        held_in = lax.dynamic_index_in_dim(stash_in, read_slot, 0, keepdims=False)
        held_pre = lax.dynamic_index_in_dim(stash_pre, read_slot, 0, keepdims=False)
        grad_in = jnp.where(is_last, top_grad, recv_grad)

        def run_bwd(bwd_args):
            return stage_backward(bwd_args[0], held_in, held_pre, w_in_list, w_out_list, bwd_args[1], bwd_args[2])

        def skip_bwd(bwd_args):
            return bwd_args

        grad_out, acc_in, acc_out = lax.cond(bwd_ok, run_bwd, skip_bwd, (grad_in, acc_in, acc_out))
        recv_act = lax.ppermute(act_out, 'stage', fwd_pairs)
        recv_grad = lax.ppermute(grad_out, 'stage', bwd_pairs)
        return (recv_act, recv_grad, stash_in, stash_pre, acc_in, acc_out, loss_acc)

    start_state = (
        jnp.zeros((tok_rows, d_model), jnp.bfloat16),
        jnp.zeros((tok_rows, d_model), jnp.bfloat16),
        jnp.zeros((stash_slots + 1, layers, tok_rows, d_model), jnp.bfloat16),
        jnp.zeros((stash_slots + 1, layers, tok_rows, 4 * d_model), jnp.bfloat16),
        [jnp.zeros((d_model, 4 * d_model), jnp.float32) for _ in range(layers)],
        [jnp.zeros((4 * d_model, d_model), jnp.float32) for _ in range(layers)],
        jnp.zeros((), jnp.float32),
    )
    end_state = lax.fori_loop(0, tick_count, tick_body, start_state)
    acc_in = end_state[4]
    acc_out = end_state[5]
    grad_local = jnp.stack([jnp.concatenate([acc_in[layer_idx].reshape(-1), acc_out[layer_idx].reshape(-1)]) for layer_idx in range(layers)])[None]
    return grad_local, end_state[6], token_count


def adam_update(w_master, m_prior, v_prior, grad_part, clip_scale, d_model):
    scaled = clip_scale * grad_part
    m_new = ADAM_BETA1 * m_prior + (1.0 - ADAM_BETA1) * scaled
    v_new = ADAM_BETA2 * v_prior + (1.0 - ADAM_BETA2) * scaled * scaled
    m_hat = m_new / (1.0 - ADAM_BETA1 ** ADAM_STEP)
    v_hat = v_new / (1.0 - ADAM_BETA2 ** ADAM_STEP)
    learn_rate = LR_BASE / math.sqrt(d_model)
    w_new = w_master - learn_rate * (m_hat / (jnp.sqrt(v_hat) + ADAM_EPS) + WEIGHT_DECAY * w_master)
    return w_new, m_new, v_new


def solution(mesh):
    stages = mesh.shape['stage']
    data_size = mesh.shape['data']

    def device_step(x_in, targets, w_work, w_master, m_prior, v_prior, clip_tau):
        grad_local, loss_acc, token_count = run_stages(x_in, targets, w_work, stages, data_size)
        grad_part = lax.psum_scatter(grad_local, 'data', scatter_dimension=2, tiled=True)
        sq_total = lax.psum(jnp.sum(grad_part * grad_part), ('stage', 'data'))
        clip_scale = jnp.minimum(1.0, clip_tau / jnp.sqrt(sq_total))
        w_new, m_new, v_new = adam_update(w_master, m_prior, v_prior, grad_part, clip_scale, x_in.shape[-1])
        w_bf16 = lax.all_gather(w_new.astype(jnp.bfloat16), 'data', axis=2, tiled=True)
        loss_mean = lax.psum(loss_acc, ('stage', 'data')) / token_count
        return loss_mean, w_bf16, w_new, m_new, v_new

    row_spec = P(None, 'data', None)
    shard_spec = P('stage', None, 'data')
    stage_spec = P('stage', None, None)
    return jax.shard_map(device_step, mesh=mesh, in_specs=(row_spec, row_spec, stage_spec, shard_spec, shard_spec, shard_spec, P()), out_specs=(P(), stage_spec, shard_spec, shard_spec, shard_spec), check_vma=False)
```

profile of v0, /device:TPU:0, one launch (start us, length us, event | category | flops | bytes accessed | tf_op | source)
XLA Modules:
  0.0 6533.0 jit_solution(13850846664778878923)
XLA Ops:
  7.2 184.6 %slice_reduce_fusion = (bf16[4194304]{0:T(1024)(128)(2,1)}, bf16[4194304]{0:T(1024)(128)(2,1)}) fusion(bf16[1,1,8388608]{2,1,0:T(2,128)(2,1)} %param.15), kind=kLoop, calls=%fused_computation.59 | loop fusion | bytes 33554432 | tf_op jit(solution)/shard_map/slice | solution.py:21
  218.4 51.0 broadcast_in_dim.39
  308.1 5656.4 %while.27 = (s32[]{:T(128)}, bf16[4096,1024]{1,0:T(8,128)(2,1)}, bf16[4096,1024]{1,0:T(8,128)(2,1)}, bf16[5,1,4096,1024]{3,2,1,0:T(8,128)(2,1)}, bf16[5,1,4096,4...) while((s32[]{:T(128)}, bf16[4096,1024]{1,0:T(8,128)(2,1)}, ...), condition=%wide.region_6.7_spmd, body=%wide.region_0.6_spmd.sunk | while | flops 206946959360 | bytes 629146432 | solution.py:117
  316.0 93.4 %conditional.4 = (bf16[4096,1024]{1,0:T(8,128)(2,1)}, bf16[1,1,4096,4096]{3,2,1,0:T(8,128)(2,1)}, bf16[1,1,4096,1024]{3,2,1,0:T(8,128)(2,1)}) conditional(s32[]{:T(128)} %convert_element_type.170, bf16[4096,1024]{1,0:T(8,128)(2,1)} %bitcast_select_fusion.2, (bf16[4096,1024]{1,0:T(8,128)(2,1)}, bf16[1024,4096]{1,0:T(8,128)(2,1)}, ...), branch_computations={%region_1.1_spmd, %region_2.2_spmd} | conditional | flops 68916609024 | bytes 109051928 | solution.py:82
  316.0 43.1 convolution_convert_fusion
  359.1 50.1 add_convert_fusion
  485.5 164.8 %collective-permute-done.1 = bf16[4096,1024]{1,0:T(8,128)(2,1)} collective-permute-done((bf16[4096,1024]{1,0:T(8,128)(2,1)}, bf16[4096,1024]{1,0:T(8,128)(2,1)}, u32[]{:S(2)}, u32[]{:S(2)}) %collective-permute-start.1) | collective-permute-done | bytes 8388640 | tf_op jit(solution)/shard_map/while/body/eval_jaxpr/ppermute | solution.py:105
  658.9 93.4 %conditional.4 = (bf16[4096,1024]{1,0:T(8,128)(2,1)}, bf16[1,1,4096,4096]{3,2,1,0:T(8,128)(2,1)}, bf16[1,1,4096,1024]{3,2,1,0:T(8,128)(2,1)}) conditional(s32[]{:T(128)} %convert_element_type.170, bf16[4096,1024]{1,0:T(8,128)(2,1)} %bitcast_select_fusion.2, (bf16[4096,1024]{1,0:T(8,128)(2,1)}, bf16[1024,4096]{1,0:T(8,128)(2,1)}, ...), branch_computations={%region_1.1_spmd, %region_2.2_spmd} | conditional | flops 68916609024 | bytes 109051928 | solution.py:82
  658.9 43.1 convolution_convert_fusion
  702.0 50.1 add_convert_fusion
  809.4 185.4 %collective-permute-start = (bf16[4096,1024]{1,0:T(8,128)(2,1)}, bf16[4096,1024]{1,0:T(8,128)(2,1)}, u32[]{:S(2)}, u32[]{:S(2)}) collective-permute-start(bf16[4096,1024]{1,0:T(8,128)(2,1)} %get-tuple-element.699), channel_id=1, source_target_pairs={{0,2},{2,4},{4,6},{1,3},{3,5},{5,7}} | collective-permute-start | bytes 25165832 | tf_op jit(solution)/shard_map/while/body/eval_jaxpr/ppermute | solution.py:104
  1006.2 164.8 %collective-permute-done.1 = bf16[4096,1024]{1,0:T(8,128)(2,1)} collective-permute-done((bf16[4096,1024]{1,0:T(8,128)(2,1)}, bf16[4096,1024]{1,0:T(8,128)(2,1)}, u32[]{:S(2)}, u32[]{:S(2)}) %collective-permute-start.1) | collective-permute-done | bytes 8388640 | tf_op jit(solution)/shard_map/while/body/eval_jaxpr/ppermute | solution.py:105
  1178.7 93.7 %conditional.4 = (bf16[4096,1024]{1,0:T(8,128)(2,1)}, bf16[1,1,4096,4096]{3,2,1,0:T(8,128)(2,1)}, bf16[1,1,4096,1024]{3,2,1,0:T(8,128)(2,1)}) conditional(s32[]{:T(128)} %convert_element_type.170, bf16[4096,1024]{1,0:T(8,128)(2,1)} %bitcast_select_fusion.2, (bf16[4096,1024]{1,0:T(8,128)(2,1)}, bf16[1024,4096]{1,0:T(8,128)(2,1)}, ...), branch_computations={%region_1.1_spmd, %region_2.2_spmd} | conditional | flops 68916609024 | bytes 109051928 | solution.py:82
  1178.7 43.1 convolution_convert_fusion
  1221.8 50.1 add_convert_fusion
  1329.3 185.8 %collective-permute-start = (bf16[4096,1024]{1,0:T(8,128)(2,1)}, bf16[4096,1024]{1,0:T(8,128)(2,1)}, u32[]{:S(2)}, u32[]{:S(2)}) collective-permute-start(bf16[4096,1024]{1,0:T(8,128)(2,1)} %get-tuple-element.699), channel_id=1, source_target_pairs={{0,2},{2,4},{4,6},{1,3},{3,5},{5,7}} | collective-permute-start | bytes 25165832 | tf_op jit(solution)/shard_map/while/body/eval_jaxpr/ppermute | solution.py:104
  1526.5 164.8 %collective-permute-done.1 = bf16[4096,1024]{1,0:T(8,128)(2,1)} collective-permute-done((bf16[4096,1024]{1,0:T(8,128)(2,1)}, bf16[4096,1024]{1,0:T(8,128)(2,1)}, u32[]{:S(2)}, u32[]{:S(2)}) %collective-permute-start.1) | collective-permute-done | bytes 8388640 | tf_op jit(solution)/shard_map/while/body/eval_jaxpr/ppermute | solution.py:105
  1698.9 93.6 %conditional.4 = (bf16[4096,1024]{1,0:T(8,128)(2,1)}, bf16[1,1,4096,4096]{3,2,1,0:T(8,128)(2,1)}, bf16[1,1,4096,1024]{3,2,1,0:T(8,128)(2,1)}) conditional(s32[]{:T(128)} %convert_element_type.170, bf16[4096,1024]{1,0:T(8,128)(2,1)} %bitcast_select_fusion.2, (bf16[4096,1024]{1,0:T(8,128)(2,1)}, bf16[1024,4096]{1,0:T(8,128)(2,1)}, ...), branch_computations={%region_1.1_spmd, %region_2.2_spmd} | conditional | flops 68916609024 | bytes 109051928 | solution.py:82
  1698.9 43.1 convolution_convert_fusion
  1742.0 50.4 add_convert_fusion
  1849.5 185.4 %collective-permute-start = (bf16[4096,1024]{1,0:T(8,128)(2,1)}, bf16[4096,1024]{1,0:T(8,128)(2,1)}, u32[]{:S(2)}, u32[]{:S(2)}) collective-permute-start(bf16[4096,1024]{1,0:T(8,128)(2,1)} %get-tuple-element.699), channel_id=1, source_target_pairs={{0,2},{2,4},{4,6},{1,3},{3,5},{5,7}} | collective-permute-start | bytes 25165832 | tf_op jit(solution)/shard_map/while/body/eval_jaxpr/ppermute | solution.py:104
  2046.2 164.8 %collective-permute-done.1 = bf16[4096,1024]{1,0:T(8,128)(2,1)} collective-permute-done((bf16[4096,1024]{1,0:T(8,128)(2,1)}, bf16[4096,1024]{1,0:T(8,128)(2,1)}, u32[]{:S(2)}, u32[]{:S(2)}) %collective-permute-start.1) | collective-permute-done | bytes 8388640 | tf_op jit(solution)/shard_map/while/body/eval_jaxpr/ppermute | solution.py:105
  2218.8 26.5 conditional.4
  2302.4 251.5 %collective-permute-start = (bf16[4096,1024]{1,0:T(8,128)(2,1)}, bf16[4096,1024]{1,0:T(8,128)(2,1)}, u32[]{:S(2)}, u32[]{:S(2)}) collective-permute-start(bf16[4096,1024]{1,0:T(8,128)(2,1)} %get-tuple-element.699), channel_id=1, source_target_pairs={{0,2},{2,4},{4,6},{1,3},{3,5},{5,7}} | collective-permute-start | bytes 25165832 | tf_op jit(solution)/shard_map/while/body/eval_jaxpr/ppermute | solution.py:104
  2565.3 161.6 %collective-permute-done.1 = bf16[4096,1024]{1,0:T(8,128)(2,1)} collective-permute-done((bf16[4096,1024]{1,0:T(8,128)(2,1)}, bf16[4096,1024]{1,0:T(8,128)(2,1)}, u32[]{:S(2)}, u32[]{:S(2)}) %collective-permute-start.1) | collective-permute-done | bytes 8388640 | tf_op jit(solution)/shard_map/while/body/eval_jaxpr/ppermute | solution.py:105
  2735.6 26.6 conditional.4
  2819.0 450.6 %collective-permute-start = (bf16[4096,1024]{1,0:T(8,128)(2,1)}, bf16[4096,1024]{1,0:T(8,128)(2,1)}, u32[]{:S(2)}, u32[]{:S(2)}) collective-permute-start(bf16[4096,1024]{1,0:T(8,128)(2,1)} %get-tuple-element.699), channel_id=1, source_target_pairs={{0,2},{2,4},{4,6},{1,3},{3,5},{5,7}} | collective-permute-start | bytes 25165832 | tf_op jit(solution)/shard_map/while/body/eval_jaxpr/ppermute | solution.py:104
  3281.0 159.5 %collective-permute-done.1 = bf16[4096,1024]{1,0:T(8,128)(2,1)} collective-permute-done((bf16[4096,1024]{1,0:T(8,128)(2,1)}, bf16[4096,1024]{1,0:T(8,128)(2,1)}, u32[]{:S(2)}, u32[]{:S(2)}) %collective-permute-start.1) | collective-permute-done | bytes 8388640 | tf_op jit(solution)/shard_map/while/body/eval_jaxpr/ppermute | solution.py:105
  3449.0 26.8 conditional.4
  3519.6 216.0 %conditional.5 = (bf16[4096,1024]{1,0:T(8,128)(2,1)}, f32[1024,4096]{1,0:T(8,128)}, f32[4096,1024]{1,0:T(8,128)}) conditional(s32[]{:T(128)} %convert_element_type.171, (bf16[4096,1024]{1,0:T(8,128)(2,1)}, f32[1024,4096]{1,0:T(8,128)}, f32[4096,1024]{1,0:T(8,128)}) %tuple.86, (bf16[4096,1024]{1,0:T(8,128)(2,1)}, bf16[4096,1024]{1,0:T(8,128)(2,1)}, ...), branch_computations={%region_3.3_spmd, %region_4.4_spmd} | conditional | flops 137980018688 | bytes 293601440 | solution.py:103
  3519.7 84.9 %fusion.17 = bf16[4096,4096]{1,0:T(8,128)(2,1)} fusion(bf16[4096,1024]{1,0:T(8,128)(2,1)} %get-tuple-element.514, bf16[4096,1024]{1,0:T(8,128)(2,1)} %get-tuple-element.515, bf16[5,1,4096,4096]{3,2,1,0:T(8,128)(2,1)} %get-tuple-element.516, s32[]{:T(128)S(6)} %select_n.124), kind=kOutput, calls=%fused_computation.25 | convolution fusion | flops 34712059904 | bytes 83886080 | tf_op jit(solution)/shard_map/while/body/eval_jaxpr/cond/branch_1_fun/nk,fk->nf/dot_general | solution.py:42
  3604.6 43.2 fusion.33
  3647.8 42.9 add_convert_fusion.1
  3690.7 44.4 fusion.27
  3736.8 256.1 %collective-permute-start = (bf16[4096,1024]{1,0:T(8,128)(2,1)}, bf16[4096,1024]{1,0:T(8,128)(2,1)}, u32[]{:S(2)}, u32[]{:S(2)}) collective-permute-start(bf16[4096,1024]{1,0:T(8,128)(2,1)} %get-tuple-element.699), channel_id=1, source_target_pairs={{0,2},{2,4},{4,6},{1,3},{3,5},{5,7}} | collective-permute-start | bytes 25165832 | tf_op jit(solution)/shard_map/while/body/eval_jaxpr/ppermute | solution.py:104
  4004.3 158.6 %collective-permute-done.1 = bf16[4096,1024]{1,0:T(8,128)(2,1)} collective-permute-done((bf16[4096,1024]{1,0:T(8,128)(2,1)}, bf16[4096,1024]{1,0:T(8,128)(2,1)}, u32[]{:S(2)}, u32[]{:S(2)}) %collective-permute-start.1) | collective-permute-done | bytes 8388640 | tf_op jit(solution)/shard_map/while/body/eval_jaxpr/ppermute | solution.py:105
  4171.3 26.6 conditional.4
  4241.7 216.0 %conditional.5 = (bf16[4096,1024]{1,0:T(8,128)(2,1)}, f32[1024,4096]{1,0:T(8,128)}, f32[4096,1024]{1,0:T(8,128)}) conditional(s32[]{:T(128)} %convert_element_type.171, (bf16[4096,1024]{1,0:T(8,128)(2,1)}, f32[1024,4096]{1,0:T(8,128)}, f32[4096,1024]{1,0:T(8,128)}) %tuple.86, (bf16[4096,1024]{1,0:T(8,128)(2,1)}, bf16[4096,1024]{1,0:T(8,128)(2,1)}, ...), branch_computations={%region_3.3_spmd, %region_4.4_spmd} | conditional | flops 137980018688 | bytes 293601440 | solution.py:103
  4242.2 84.9 %fusion.17 = bf16[4096,4096]{1,0:T(8,128)(2,1)} fusion(bf16[4096,1024]{1,0:T(8,128)(2,1)} %get-tuple-element.514, bf16[4096,1024]{1,0:T(8,128)(2,1)} %get-tuple-element.515, bf16[5,1,4096,4096]{3,2,1,0:T(8,128)(2,1)} %get-tuple-element.516, s32[]{:T(128)S(6)} %select_n.124), kind=kOutput, calls=%fused_computation.25 | convolution fusion | flops 34712059904 | bytes 83886080 | tf_op jit(solution)/shard_map/while/body/eval_jaxpr/cond/branch_1_fun/nk,fk->nf/dot_general | solution.py:42
  4327.1 43.1 fusion.33
  4370.2 42.9 add_convert_fusion.1
  4413.1 44.4 fusion.27
  4459.0 188.1 %collective-permute-start = (bf16[4096,1024]{1,0:T(8,128)(2,1)}, bf16[4096,1024]{1,0:T(8,128)(2,1)}, u32[]{:S(2)}, u32[]{:S(2)}) collective-permute-start(bf16[4096,1024]{1,0:T(8,128)(2,1)} %get-tuple-element.699), channel_id=1, source_target_pairs={{0,2},{2,4},{4,6},{1,3},{3,5},{5,7}} | collective-permute-start | bytes 25165832 | tf_op jit(solution)/shard_map/while/body/eval_jaxpr/ppermute | solution.py:104
  4658.5 157.7 %collective-permute-done.1 = bf16[4096,1024]{1,0:T(8,128)(2,1)} collective-permute-done((bf16[4096,1024]{1,0:T(8,128)(2,1)}, bf16[4096,1024]{1,0:T(8,128)(2,1)}, u32[]{:S(2)}, u32[]{:S(2)}) %collective-permute-start.1) | collective-permute-done | bytes 8388640 | tf_op jit(solution)/shard_map/while/body/eval_jaxpr/ppermute | solution.py:105
  4824.9 26.8 conditional.4
  4895.6 216.1 %conditional.5 = (bf16[4096,1024]{1,0:T(8,128)(2,1)}, f32[1024,4096]{1,0:T(8,128)}, f32[4096,1024]{1,0:T(8,128)}) conditional(s32[]{:T(128)} %convert_element_type.171, (bf16[4096,1024]{1,0:T(8,128)(2,1)}, f32[1024,4096]{1,0:T(8,128)}, f32[4096,1024]{1,0:T(8,128)}) %tuple.86, (bf16[4096,1024]{1,0:T(8,128)(2,1)}, bf16[4096,1024]{1,0:T(8,128)(2,1)}, ...), branch_computations={%region_3.3_spmd, %region_4.4_spmd} | conditional | flops 137980018688 | bytes 293601440 | solution.py:103
  4895.8 84.9 %fusion.17 = bf16[4096,4096]{1,0:T(8,128)(2,1)} fusion(bf16[4096,1024]{1,0:T(8,128)(2,1)} %get-tuple-element.514, bf16[4096,1024]{1,0:T(8,128)(2,1)} %get-tuple-element.515, bf16[5,1,4096,4096]{3,2,1,0:T(8,128)(2,1)} %get-tuple-element.516, s32[]{:T(128)S(6)} %select_n.124), kind=kOutput, calls=%fused_computation.25 | convolution fusion | flops 34712059904 | bytes 83886080 | tf_op jit(solution)/shard_map/while/body/eval_jaxpr/cond/branch_1_fun/nk,fk->nf/dot_general | solution.py:42
  4980.6 43.2 fusion.33
  5023.8 42.9 add_convert_fusion.1
  5066.7 44.5 fusion.27
  5113.0 189.2 %collective-permute-start = (bf16[4096,1024]{1,0:T(8,128)(2,1)}, bf16[4096,1024]{1,0:T(8,128)(2,1)}, u32[]{:S(2)}, u32[]{:S(2)}) collective-permute-start(bf16[4096,1024]{1,0:T(8,128)(2,1)} %get-tuple-element.699), channel_id=1, source_target_pairs={{0,2},{2,4},{4,6},{1,3},{3,5},{5,7}} | collective-permute-start | bytes 25165832 | tf_op jit(solution)/shard_map/while/body/eval_jaxpr/ppermute | solution.py:104
  5313.6 164.8 %collective-permute-done.1 = bf16[4096,1024]{1,0:T(8,128)(2,1)} collective-permute-done((bf16[4096,1024]{1,0:T(8,128)(2,1)}, bf16[4096,1024]{1,0:T(8,128)(2,1)}, u32[]{:S(2)}, u32[]{:S(2)}) %collective-permute-start.1) | collective-permute-done | bytes 8388640 | tf_op jit(solution)/shard_map/while/body/eval_jaxpr/ppermute | solution.py:105
  5485.9 26.6 conditional.4
  5556.3 216.0 %conditional.5 = (bf16[4096,1024]{1,0:T(8,128)(2,1)}, f32[1024,4096]{1,0:T(8,128)}, f32[4096,1024]{1,0:T(8,128)}) conditional(s32[]{:T(128)} %convert_element_type.171, (bf16[4096,1024]{1,0:T(8,128)(2,1)}, f32[1024,4096]{1,0:T(8,128)}, f32[4096,1024]{1,0:T(8,128)}) %tuple.86, (bf16[4096,1024]{1,0:T(8,128)(2,1)}, bf16[4096,1024]{1,0:T(8,128)(2,1)}, ...), branch_computations={%region_3.3_spmd, %region_4.4_spmd} | conditional | flops 137980018688 | bytes 293601440 | solution.py:103
  5556.7 84.9 %fusion.17 = bf16[4096,4096]{1,0:T(8,128)(2,1)} fusion(bf16[4096,1024]{1,0:T(8,128)(2,1)} %get-tuple-element.514, bf16[4096,1024]{1,0:T(8,128)(2,1)} %get-tuple-element.515, bf16[5,1,4096,4096]{3,2,1,0:T(8,128)(2,1)} %get-tuple-element.516, s32[]{:T(128)S(6)} %select_n.124), kind=kOutput, calls=%fused_computation.25 | convolution fusion | flops 34712059904 | bytes 83886080 | tf_op jit(solution)/shard_map/while/body/eval_jaxpr/cond/branch_1_fun/nk,fk->nf/dot_general | solution.py:42
  5641.6 43.1 fusion.33
  5684.7 42.9 add_convert_fusion.1
  5727.6 44.4 fusion.27
  5792.6 164.8 %collective-permute-done.1 = bf16[4096,1024]{1,0:T(8,128)(2,1)} collective-permute-done((bf16[4096,1024]{1,0:T(8,128)(2,1)}, bf16[4096,1024]{1,0:T(8,128)(2,1)}, u32[]{:S(2)}, u32[]{:S(2)}) %collective-permute-start.1) | collective-permute-done | bytes 8388640 | tf_op jit(solution)/shard_map/while/body/eval_jaxpr/ppermute | solution.py:105
  6015.8 245.0 %all-reduce.4.cloned.1.call-done = f32[1,1,8388608]{2,1,0:T(1,128)} async-done(((f32[1,1,8388608]{2,1,0:T(1,128)}), f32[1,1,8388608]{2,1,0:T(1,128)}) %all-reduce.4.cloned.1.call-update) | async-done | bytes 33554448
  6260.8 36.3 multiply_reduce_fusion.1
  6322.1 115.6 %fusion.44 = (bf16[1,1,4194304]{2,1,0:T(2,128)(2,1)}, f32[1,1,4194304]{2,1,0:T(1,128)}, f32[1,1,4194304]{2,1,0:T(1,128)}, f32[1,1,4194304]{2,1,0:T(1,128)}) fusion(f32[1,1,4194304]{2,1,0:T(1,128)} %param.16, f32[1,1,8388608]{2,1,0:T(1,128)} %all-reduce.4.cloned.1.call-done, u32[]{:T(128)S(6)} %multiply.17, f32[]{:T(128)S(6)} %min.26, ...), kind=kLoop, calls=%fused_computation.61 | loop fusion | flops 71303168 | bytes 125829128 | tf_op jit(solution)/shard_map/convert_element_type | solution.py:145
  6438.4 48.7 all-gather.2.cloned.1.call-done
  6487.0 37.8 copy.57
  (122 shorter events, 1047.5 us)
Async XLA Ops:
  7.2 6253.6 %all-reduce.4.cloned.1.call-start = ((), (), s32[]{:S(2)}) async-start(), calls=%async_computation.1 | async-start | bytes 67108864
  465.1 185.2 %collective-permute-start.1 = (bf16[4096,1024]{1,0:T(8,128)(2,1)}, bf16[4096,1024]{1,0:T(8,128)(2,1)}, u32[]{:S(2)}, u32[]{:S(2)}) collective-permute-start(bf16[4096,1024]{1,0:T(8,128)(2,1)} %get-tuple-element.702), channel_id=1, source_target_pairs={{2,0},{4,2},{6,4},{3,1},{5,3},{7,5}} | collective-permute-start | bytes 25165832 | tf_op jit(solution)/shard_map/while/body/eval_jaxpr/ppermute | solution.py:105
  466.4 185.0 %collective-permute-start = (bf16[4096,1024]{1,0:T(8,128)(2,1)}, bf16[4096,1024]{1,0:T(8,128)(2,1)}, u32[]{:S(2)}, u32[]{:S(2)}) collective-permute-start(bf16[4096,1024]{1,0:T(8,128)(2,1)} %get-tuple-element.699), channel_id=1, source_target_pairs={{0,2},{2,4},{4,6},{1,3},{3,5},{5,7}} | collective-permute-start | bytes 25165832 | tf_op jit(solution)/shard_map/while/body/eval_jaxpr/ppermute | solution.py:104
  808.1 362.9 %collective-permute-start.1 = (bf16[4096,1024]{1,0:T(8,128)(2,1)}, bf16[4096,1024]{1,0:T(8,128)(2,1)}, u32[]{:S(2)}, u32[]{:S(2)}) collective-permute-start(bf16[4096,1024]{1,0:T(8,128)(2,1)} %get-tuple-element.702), channel_id=1, source_target_pairs={{2,0},{4,2},{6,4},{3,1},{5,3},{7,5}} | collective-permute-start | bytes 25165832 | tf_op jit(solution)/shard_map/while/body/eval_jaxpr/ppermute | solution.py:105
  809.4 362.0 %collective-permute-start = (bf16[4096,1024]{1,0:T(8,128)(2,1)}, bf16[4096,1024]{1,0:T(8,128)(2,1)}, u32[]{:S(2)}, u32[]{:S(2)}) collective-permute-start(bf16[4096,1024]{1,0:T(8,128)(2,1)} %get-tuple-element.699), channel_id=1, source_target_pairs={{0,2},{2,4},{4,6},{1,3},{3,5},{5,7}} | collective-permute-start | bytes 25165832 | tf_op jit(solution)/shard_map/while/body/eval_jaxpr/ppermute | solution.py:104
  1328.0 363.3 %collective-permute-start.1 = (bf16[4096,1024]{1,0:T(8,128)(2,1)}, bf16[4096,1024]{1,0:T(8,128)(2,1)}, u32[]{:S(2)}, u32[]{:S(2)}) collective-permute-start(bf16[4096,1024]{1,0:T(8,128)(2,1)} %get-tuple-element.702), channel_id=1, source_target_pairs={{2,0},{4,2},{6,4},{3,1},{5,3},{7,5}} | collective-permute-start | bytes 25165832 | tf_op jit(solution)/shard_map/while/body/eval_jaxpr/ppermute | solution.py:105
  1329.3 362.0 %collective-permute-start = (bf16[4096,1024]{1,0:T(8,128)(2,1)}, bf16[4096,1024]{1,0:T(8,128)(2,1)}, u32[]{:S(2)}, u32[]{:S(2)}) collective-permute-start(bf16[4096,1024]{1,0:T(8,128)(2,1)} %get-tuple-element.699), channel_id=1, source_target_pairs={{0,2},{2,4},{4,6},{1,3},{3,5},{5,7}} | collective-permute-start | bytes 25165832 | tf_op jit(solution)/shard_map/while/body/eval_jaxpr/ppermute | solution.py:104
  1848.2 362.8 %collective-permute-start.1 = (bf16[4096,1024]{1,0:T(8,128)(2,1)}, bf16[4096,1024]{1,0:T(8,128)(2,1)}, u32[]{:S(2)}, u32[]{:S(2)}) collective-permute-start(bf16[4096,1024]{1,0:T(8,128)(2,1)} %get-tuple-element.702), channel_id=1, source_target_pairs={{2,0},{4,2},{6,4},{3,1},{5,3},{7,5}} | collective-permute-start | bytes 25165832 | tf_op jit(solution)/shard_map/while/body/eval_jaxpr/ppermute | solution.py:105
  1849.5 361.5 %collective-permute-start = (bf16[4096,1024]{1,0:T(8,128)(2,1)}, bf16[4096,1024]{1,0:T(8,128)(2,1)}, u32[]{:S(2)}, u32[]{:S(2)}) collective-permute-start(bf16[4096,1024]{1,0:T(8,128)(2,1)} %get-tuple-element.699), channel_id=1, source_target_pairs={{0,2},{2,4},{4,6},{1,3},{3,5},{5,7}} | collective-permute-start | bytes 25165832 | tf_op jit(solution)/shard_map/while/body/eval_jaxpr/ppermute | solution.py:104
  2301.1 425.8 %collective-permute-start.1 = (bf16[4096,1024]{1,0:T(8,128)(2,1)}, bf16[4096,1024]{1,0:T(8,128)(2,1)}, u32[]{:S(2)}, u32[]{:S(2)}) collective-permute-start(bf16[4096,1024]{1,0:T(8,128)(2,1)} %get-tuple-element.702), channel_id=1, source_target_pairs={{2,0},{4,2},{6,4},{3,1},{5,3},{7,5}} | collective-permute-start | bytes 25165832 | tf_op jit(solution)/shard_map/while/body/eval_jaxpr/ppermute | solution.py:105
  2302.4 425.7 %collective-permute-start = (bf16[4096,1024]{1,0:T(8,128)(2,1)}, bf16[4096,1024]{1,0:T(8,128)(2,1)}, u32[]{:S(2)}, u32[]{:S(2)}) collective-permute-start(bf16[4096,1024]{1,0:T(8,128)(2,1)} %get-tuple-element.699), channel_id=1, source_target_pairs={{0,2},{2,4},{4,6},{1,3},{3,5},{5,7}} | collective-permute-start | bytes 25165832 | tf_op jit(solution)/shard_map/while/body/eval_jaxpr/ppermute | solution.py:104
  2817.7 622.8 %collective-permute-start.1 = (bf16[4096,1024]{1,0:T(8,128)(2,1)}, bf16[4096,1024]{1,0:T(8,128)(2,1)}, u32[]{:S(2)}, u32[]{:S(2)}) collective-permute-start(bf16[4096,1024]{1,0:T(8,128)(2,1)} %get-tuple-element.702), channel_id=1, source_target_pairs={{2,0},{4,2},{6,4},{3,1},{5,3},{7,5}} | collective-permute-start | bytes 25165832 | tf_op jit(solution)/shard_map/while/body/eval_jaxpr/ppermute | solution.py:105
  2819.0 622.6 %collective-permute-start = (bf16[4096,1024]{1,0:T(8,128)(2,1)}, bf16[4096,1024]{1,0:T(8,128)(2,1)}, u32[]{:S(2)}, u32[]{:S(2)}) collective-permute-start(bf16[4096,1024]{1,0:T(8,128)(2,1)} %get-tuple-element.699), channel_id=1, source_target_pairs={{0,2},{2,4},{4,6},{1,3},{3,5},{5,7}} | collective-permute-start | bytes 25165832 | tf_op jit(solution)/shard_map/while/body/eval_jaxpr/ppermute | solution.py:104
  3735.5 427.4 %collective-permute-start.1 = (bf16[4096,1024]{1,0:T(8,128)(2,1)}, bf16[4096,1024]{1,0:T(8,128)(2,1)}, u32[]{:S(2)}, u32[]{:S(2)}) collective-permute-start(bf16[4096,1024]{1,0:T(8,128)(2,1)} %get-tuple-element.702), channel_id=1, source_target_pairs={{2,0},{4,2},{6,4},{3,1},{5,3},{7,5}} | collective-permute-start | bytes 25165832 | tf_op jit(solution)/shard_map/while/body/eval_jaxpr/ppermute | solution.py:105
  3736.8 427.0 %collective-permute-start = (bf16[4096,1024]{1,0:T(8,128)(2,1)}, bf16[4096,1024]{1,0:T(8,128)(2,1)}, u32[]{:S(2)}, u32[]{:S(2)}) collective-permute-start(bf16[4096,1024]{1,0:T(8,128)(2,1)} %get-tuple-element.699), channel_id=1, source_target_pairs={{0,2},{2,4},{4,6},{1,3},{3,5},{5,7}} | collective-permute-start | bytes 25165832 | tf_op jit(solution)/shard_map/while/body/eval_jaxpr/ppermute | solution.py:104
  4457.7 358.5 %collective-permute-start.1 = (bf16[4096,1024]{1,0:T(8,128)(2,1)}, bf16[4096,1024]{1,0:T(8,128)(2,1)}, u32[]{:S(2)}, u32[]{:S(2)}) collective-permute-start(bf16[4096,1024]{1,0:T(8,128)(2,1)} %get-tuple-element.702), channel_id=1, source_target_pairs={{2,0},{4,2},{6,4},{3,1},{5,3},{7,5}} | collective-permute-start | bytes 25165832 | tf_op jit(solution)/shard_map/while/body/eval_jaxpr/ppermute | solution.py:105
  4459.0 358.3 %collective-permute-start = (bf16[4096,1024]{1,0:T(8,128)(2,1)}, bf16[4096,1024]{1,0:T(8,128)(2,1)}, u32[]{:S(2)}, u32[]{:S(2)}) collective-permute-start(bf16[4096,1024]{1,0:T(8,128)(2,1)} %get-tuple-element.699), channel_id=1, source_target_pairs={{0,2},{2,4},{4,6},{1,3},{3,5},{5,7}} | collective-permute-start | bytes 25165832 | tf_op jit(solution)/shard_map/while/body/eval_jaxpr/ppermute | solution.py:104
  5111.7 366.7 %collective-permute-start.1 = (bf16[4096,1024]{1,0:T(8,128)(2,1)}, bf16[4096,1024]{1,0:T(8,128)(2,1)}, u32[]{:S(2)}, u32[]{:S(2)}) collective-permute-start(bf16[4096,1024]{1,0:T(8,128)(2,1)} %get-tuple-element.702), channel_id=1, source_target_pairs={{2,0},{4,2},{6,4},{3,1},{5,3},{7,5}} | collective-permute-start | bytes 25165832 | tf_op jit(solution)/shard_map/while/body/eval_jaxpr/ppermute | solution.py:105
  5113.0 365.4 %collective-permute-start = (bf16[4096,1024]{1,0:T(8,128)(2,1)}, bf16[4096,1024]{1,0:T(8,128)(2,1)}, u32[]{:S(2)}, u32[]{:S(2)}) collective-permute-start(bf16[4096,1024]{1,0:T(8,128)(2,1)} %get-tuple-element.699), channel_id=1, source_target_pairs={{0,2},{2,4},{4,6},{1,3},{3,5},{5,7}} | collective-permute-start | bytes 25165832 | tf_op jit(solution)/shard_map/while/body/eval_jaxpr/ppermute | solution.py:104
  5772.2 185.2 %collective-permute-start.1 = (bf16[4096,1024]{1,0:T(8,128)(2,1)}, bf16[4096,1024]{1,0:T(8,128)(2,1)}, u32[]{:S(2)}, u32[]{:S(2)}) collective-permute-start(bf16[4096,1024]{1,0:T(8,128)(2,1)} %get-tuple-element.702), channel_id=1, source_target_pairs={{2,0},{4,2},{6,4},{3,1},{5,3},{7,5}} | collective-permute-start | bytes 25165832 | tf_op jit(solution)/shard_map/while/body/eval_jaxpr/ppermute | solution.py:105
  5773.5 183.9 %collective-permute-start = (bf16[4096,1024]{1,0:T(8,128)(2,1)}, bf16[4096,1024]{1,0:T(8,128)(2,1)}, u32[]{:S(2)}, u32[]{:S(2)}) collective-permute-start(bf16[4096,1024]{1,0:T(8,128)(2,1)} %get-tuple-element.699), channel_id=1, source_target_pairs={{0,2},{2,4},{4,6},{1,3},{3,5},{5,7}} | collective-permute-start | bytes 25165832 | tf_op jit(solution)/shard_map/while/body/eval_jaxpr/ppermute | solution.py:104
  5964.6 16.5 copy-start
  6013.8 0.7 copy-start.1
  6013.8 473.2 %all-gather.2.cloned.1.call-start = ((), (), s32[]{:S(2)}) async-start(), calls=%async_computation | async-start | bytes 50331648 | tf_op jit(solution)/shard_map/all_gather | solution.py:145
Sparse Core Ops, SparseCore 0:
  6013.9 246.7 all-reduce.3
  6437.8 49.1 all-gather.1
where the time goes:
time: 6540 us; the launch traced here: 6530 us
  waiting for transfers between devices  1930 us (30%)
  starting transfers between devices  1920 us (29%)
  matrix products  1230 us (19%)
  local copies, waits for them, and re-layouts  851 us (13%)
  other arithmetic  492 us (8%)
  loops' own time  66.1 us (1%)
    ppermute x10, starting transfers between devices, tick_body(): recv_act = lax.ppermute(act_out, 'stage', fwd_pairs)  1910 us
    ppermute x10, waiting for transfers between devices, tick_body(): recv_grad = lax.ppermute(grad_out, 'stage', bwd_pairs)  1630 us
    dot_general x4, matrix products, stage_backward(): jnp.einsum('nk,fk->nf', grad_h, w_out_list[layer_idx], preferred_element_...  340 us
    unnamed x3, waiting for transfers between devices  245 us
    dynamic_update_slice x10, local copies, waits for them, and re-layouts, tick_body(): lax.dynamic_update_index_in_dim(stash_pre, new_pre, write_slot, 0)  228 us
    dot_general x4, matrix products, stage_forward(): jnp.dot(act_bf, w_out, preferred_element_type=jnp.float32)  201 us
    slice x1, local copies, waits for them, and re-layouts, split_layer(): w_flat[half_len:].reshape(4 * d_model, d_model)  185 us
    dot_general x4, matrix products, stage_backward(): jnp.einsum('nf,nk->fk', act_bf, grad_h, preferred_element_type=jnp.float32)  178 us
  transfers between devices with their start and end apart: 22, of which 18 were waited for; matrix products, arithmetic and copies ran while one was open for 2% of the time, Pallas kernels for 0%

commit v1 on v0

v1 whole, which is shorter than its diff:
```python
import functools
import math
import jax
import jax.numpy as jnp
from jax import lax
from jax.experimental import pallas as pl
from jax.experimental.pallas import tpu as pltpu
from jax.sharding import PartitionSpec as P

B1 = 0.9
B2 = 0.95
EPS = 1e-8
DECAY = 0.1
STEP = 10
LR_BASE = 0.05
F32 = jnp.float32
BF16 = jnp.bfloat16
K0 = math.sqrt(2.0 / math.pi)
K1 = 0.044715


def to_tiles(w):
    r, c = w.shape
    return w.reshape(r // 8, 8, c // 128, 128).transpose(0, 2, 1, 3).reshape(r * c // 1024, 8, 128)


def from_tiles(t, r, c):
    return t.reshape(r // 8, c // 128, 8, 128).transpose(0, 2, 1, 3).reshape(r, c)


def dot(a, b, dims):
    return lax.dot_general(a, b, (dims, ((), ())), preferred_element_type=F32)


def params(n):
    return pltpu.CompilerParams(dimension_semantics=('arbitrary',) * n, vmem_limit_bytes=56 * 2**20)


def cost(rows, d, f):
    return pl.CostEstimate(flops=2 * rows * d * f, bytes_accessed=80 * 2**20, transcendentals=rows * f)


def up_kernel(x_ref, w_ref, u_ref, a_ref):
    for i in range(w_ref.shape[1] // 256):
        s = (slice(None), pl.ds(i * 256, 256))
        u = dot(x_ref[...], w_ref[s], ((1,), (0,))).astype(BF16)
        u_ref[s] = u
        z = u.astype(F32)
        a_ref[s] = (z * jax.nn.sigmoid(z * (2.0 * K0 + (2.0 * K0 * K1) * (z * z)))).astype(BF16)


def up(x, stack, base):
    rows, d = x.shape
    f = 4 * d
    bm = 1024
    return pl.pallas_call(
        up_kernel,
        grid=(f // d, rows // bm),
        in_specs=[pl.BlockSpec((bm, d), lambda j, i: (i, 0)), pl.BlockSpec((d, d), lambda j, i: (base * 4 + j, 0))],
        out_specs=[pl.BlockSpec((bm, d), lambda j, i: (i, j))] * 2,
        out_shape=[jax.ShapeDtypeStruct((rows, f), BF16)] * 2,
        compiler_params=params(2), cost_estimate=cost(rows, d, f), name='up',
    )(x, stack)


def down_kernel(a_ref, w_ref, h_ref, o_ref):
    for i in range(o_ref.shape[1] // 512):
        s = (slice(None), pl.ds(i * 512, 512))
        o_ref[s] = (h_ref[s].astype(F32) + dot(a_ref[...], w_ref[s], ((1,), (0,)))).astype(BF16)


def down(a, stack, base, h):
    rows, f = a.shape
    d = h.shape[1]
    bm = 512
    return pl.pallas_call(
        down_kernel,
        grid=(rows // bm,),
        in_specs=[pl.BlockSpec((bm, f), lambda i: (i, 0)), pl.BlockSpec((f, d), lambda i: (base, 0)),
                  pl.BlockSpec((bm, d), lambda i: (i, 0))],
        out_specs=pl.BlockSpec((bm, d), lambda i: (i, 0)),
        out_shape=jax.ShapeDtypeStruct((rows, d), BF16),
        compiler_params=params(1), cost_estimate=cost(rows, d, f), name='down',
    )(a, stack, h)


def du_kernel(g_ref, w_ref, u_ref, o_ref):
    for i in range(g_ref.shape[0] // 256):
        s = pl.ds(i * 256, 256)
        e = dot(g_ref[s, :], w_ref[...], ((1,), (1,)))
        z = u_ref[s, :].astype(F32)
        zz = z * z
        p = jax.nn.sigmoid(z * (2.0 * K0 + (2.0 * K0 * K1) * zz))
        o_ref[s, :] = (e * (p + (p - p * p) * (z * (2.0 * K0 + (6.0 * K0 * K1) * zz)))).astype(BF16)


def du_of(g, stack, base, u):
    rows, d = g.shape
    f = 4 * d
    bm = 1024
    return pl.pallas_call(
        du_kernel,
        grid=(f // d, rows // bm),
        in_specs=[pl.BlockSpec((bm, d), lambda j, i: (i, 0)), pl.BlockSpec((d, d), lambda j, i: (base * 4 + j, 0)),
                  pl.BlockSpec((bm, d), lambda j, i: (i, j))],
        out_specs=pl.BlockSpec((bm, d), lambda j, i: (i, j)),
        out_shape=jax.ShapeDtypeStruct((rows, f), BF16),
        compiler_params=params(2), cost_estimate=cost(rows, d, f), name='du',
    )(g, stack, u)


def dx_kernel(u_ref, w_ref, g_ref, o_ref):
    d = o_ref.shape[1]
    acc = g_ref[...].astype(F32)
    for q in range(w_ref.shape[0] // d):
        acc = acc + dot(u_ref[:, q * d:(q + 1) * d], w_ref[pl.ds(q * d, d), :], ((1,), (1,)))
    o_ref[...] = acc.astype(BF16)


def dx(du, stack, base, g):
    rows, f = du.shape
    d = g.shape[1]
    bm = 512
    return pl.pallas_call(
        dx_kernel,
        grid=(rows // bm,),
        in_specs=[pl.BlockSpec((bm, f), lambda i: (i, 0)), pl.BlockSpec((f, d), lambda i: (base, 0)),
                  pl.BlockSpec((bm, d), lambda i: (i, 0))],
        out_specs=pl.BlockSpec((bm, d), lambda i: (i, 0)),
        out_shape=jax.ShapeDtypeStruct((rows, d), BF16),
        compiler_params=params(1), cost_estimate=cost(rows, d, f), name='dx',
    )(du, stack, g)


def adam_kernel(lr, c_ref, g_ref, w_ref, m_ref, v_ref, wo_ref, mo_ref, vo_ref, wb_ref):
    sg = c_ref[0] * g_ref[...]
    m = B1 * m_ref[...] + (1.0 - B1) * sg
    v = B2 * v_ref[...] + (1.0 - B2) * sg * sg
    mh = m * (1.0 / (1.0 - B1 ** STEP))
    vh = v * (1.0 / (1.0 - B2 ** STEP))
    w = w_ref[...]
    wn = w - lr * (mh / (jnp.sqrt(vh) + EPS) + DECAY * w)
    wo_ref[...] = wn
    mo_ref[...] = m
    vo_ref[...] = v
    wb_ref[...] = wn.astype(BF16)


def adam(c, g, w, m, v, lr):
    n = w.shape[0]
    bl = 2048
    spec = pl.BlockSpec((bl, 128), lambda i: (i, 0))
    sds = jax.ShapeDtypeStruct((n, 128), F32)
    return pl.pallas_call(
        functools.partial(adam_kernel, lr),
        grid=(n // bl,),
        in_specs=[pl.BlockSpec(memory_space=pltpu.SMEM)] + [spec] * 4,
        out_specs=[spec] * 4,
        out_shape=[sds, sds, sds, jax.ShapeDtypeStruct((n, 128), BF16)],
        compiler_params=pltpu.CompilerParams(dimension_semantics=('arbitrary',), vmem_limit_bytes=48 * 2**20),
        name='adam',
    )(c, g, w, m, v)


def solution(mesh):
    stages = mesh.shape['stage']
    swap = [(0, 1), (1, 0)]

    def device_step(x_in, targets, w_work, w_master, m_prior, v_prior, clip_tau):
        micro, rows, d = x_in.shape
        f = 4 * d
        tokens = micro * rows * 2
        stage = lax.axis_index('stage')
        core0 = lax.axis_index('data') == 0
        half = lax.optimization_barrier(w_master.reshape(-1, 128))
        mine = lax.cond(
            core0,
            lambda w: w.reshape(d, 4, d).astype(BF16).transpose(1, 0, 2).reshape(f, d),
            lambda w: w.reshape(f, d).astype(BF16),
            half)
        stack = lax.all_gather(mine, ('stage', 'data'), axis=0, tiled=True)

        h = lax.dynamic_index_in_dim(x_in, stage, 0, keepdims=False)
        t = lax.dynamic_index_in_dim(targets, stage, 0, keepdims=False)
        xs, us, acts = [], [], []
        for l in range(stages):
            xs.append(h)
            u, a = up(h, stack, 2 * l)
            h = down(a, stack, 2 * l + 1, h)
            us.append(u)
            acts.append(a)
        res = h.astype(F32) - t.astype(F32)
        loss = 0.5 * jnp.sum(res * res)
        g = (res / tokens).astype(BF16)

        parts = [None] * stages

        def dw1(o, c=None):
            m = dot(o[0], o[1], ((0,), (0,)))
            return to_tiles(m if c is None else m + from_tiles(c, d, f))

        def dw2(o, c=None):
            m = dot(o[2], o[3], ((0,), (0,)))
            return to_tiles(m if c is None else m + from_tiles(c, f, d))

        tie = lax.optimization_barrier
        for l in reversed(range(stages)):
            du = du_of(g, stack, 2 * l + 1, us[l])
            ops = (xs[l], du, acts[l], g)
            sent = lax.cond(core0, dw2, dw1, ops)
            came = lax.ppermute(sent, 'data', swap)
            if l > 0:
                g = dx(du, stack, 2 * l, g)
                came, g = tie((came, g))
            own = lax.cond(core0, dw1, dw2, ops, came)
            parts[l] = lax.psum_scatter(own, 'stage', scatter_dimension=0, tiled=True)
        sq = sum(jnp.sum(p * p) for p in parts)
        sums = lax.psum(jnp.stack([sq, loss]), ('stage', 'data'))
        gt = lax.all_to_all(jnp.stack(parts), 'stage', 0, 0)
        gt = gt.reshape(-1, 8, 128)
        grad = lax.cond(
            core0,
            lambda q: from_tiles(q, d, f).reshape(-1, 128),
            lambda q: from_tiles(q, f, d).reshape(-1, 128),
            gt)
        c = jnp.minimum(1.0, clip_tau / jnp.sqrt(sums[0]))
        w_new, m_new, v_new, wb = adam(c.reshape(1), grad, half, m_prior.reshape(-1, 128), v_prior.reshape(-1, 128), LR_BASE / math.sqrt(d))
        wb = lax.all_gather(wb.reshape(1, 1, -1), 'data', axis=2, tiled=True)
        shape = w_master.shape
        return sums[1] / tokens, wb, w_new.reshape(shape), m_new.reshape(shape), v_new.reshape(shape)

    row = P(None, 'data', None)
    shard = P('stage', None, 'data')
    whole = P('stage', None, None)
    return jax.shard_map(device_step, mesh=mesh, in_specs=(row, row, whole, shard, shard, shard, P()), out_specs=(P(), whole, shard, shard, shard), check_vma=False)
```

time: 6540 us -> 2050 us (0.31)
  starting transfers between devices: 1920 us -> 7.95 us
  waiting for transfers between devices: 1930 us -> 514 us
  matrix products: 1230 us -> 346 us
  Pallas kernels: 0 us -> 818 us
  local copies, waits for them, and re-layouts: 851 us -> 96.4 us
  other arithmetic: 492 us -> 47.8 us
  blocking collectives: 24.3 us -> 180 us
    ppermute x20 -> x4, starting transfers between devices: 1920 us -> 0.33 us  [device_step(): came = lax.ppermute(sent, 'data', swap)]
    ppermute x20 -> x4, waiting for transfers between devices: 1630 us -> 25.2 us  [device_step(): came = lax.ppermute(sent, 'data', swap)]
    dot_general x24 -> x8, matrix products: 1230 us -> 346 us  [dot(): return lax.dot_general(a, b, (dims, ((), ())), preferred_element_type=F32)]
    pallas_call x0 -> x16, Pallas kernels: none -> 818 us  [the longest x4 250 us: du_of(): pl.pallas_call(du_kernel, grid=(f // d, rows // bm), in_specs=[pl.BlockSp...]
    dynamic_update_slice x20 -> x0, local copies, waits for them, and re-layouts: 303 us -> none  [the longest x10 228 us: tick_body(): lax.dynamic_update_index_in_dim(stash_pre, new_pre, write_slot, 0)]
    all_gather x1 -> x2, waiting for transfers between devices: 48.7 us -> 341 us  [the longest x1 292 us: device_step(): stack = lax.all_gather(mine, ('stage', 'data'), axis=0, tiled=True)]
    unnamed x3 -> x6, waiting for transfers between devices: 245 us -> 0.1 us
    select_n x20 -> x0, other arithmetic: 209 us -> none  [the longest x10 135 us: tick_body(): grad_in = jnp.where(is_last, top_grad, recv_grad)]
  transfers between devices with their start and end apart: 22 -> 11, of which waited for: 18 -> 4; matrix products, arithmetic and copies ran while one was open for 2% -> 14% of each run, Pallas kernels for 0% -> 15%
where the time goes in v1:
time: 2050 us
  Pallas kernels  818 us (40%)
  waiting for transfers between devices  514 us (25%)
  matrix products  346 us (17%)
  blocking collectives  180 us (9%)
  local copies, waits for them, and re-layouts  96.4 us (5%)
  other arithmetic  47.8 us (2%)
  between operations  20.9 us (1%)
    dot_general x8, matrix products, dot(): return lax.dot_general(a, b, (dims, ((), ())), preferred_element_type=F32)  346 us
    all_gather x1, waiting for transfers between devices, device_step(): stack = lax.all_gather(mine, ('stage', 'data'), axis=0, tiled=True)  292 us
    pallas_call x4, Pallas kernels, du_of(): pl.pallas_call(du_kernel, grid=(f // d, rows // bm), in_specs=[pl.BlockSp...  250 us
    pallas_call x4, Pallas kernels, up(): pl.pallas_call(up_kernel, grid=(f // d, rows // bm), in_specs=[pl.BlockSp...  227 us
    psum x1, blocking collectives, device_step(): sums = lax.psum(jnp.stack([sq, loss]), ('stage', 'data'))  180 us
    pallas_call x4, Pallas kernels, down(): pl.pallas_call(down_kernel, grid=(rows // bm,), in_specs=[pl.BlockSpec((b...  168 us
    reduce_scatter x4, waiting for transfers between devices, device_step(): parts[l] = lax.psum_scatter(own, 'stage', scatter_dimension=0, tiled=True)  148 us
    pallas_call x3, Pallas kernels, dx(): pl.pallas_call(dx_kernel, grid=(rows // bm,), in_specs=[pl.BlockSpec((bm,...  127 us
  transfers between devices with their start and end apart: 11, of which 4 were waited for; matrix products, arithmetic and copies ran while one was open for 14% of the time, Pallas kernels for 15%

profile of v1, /device:TPU:0, one launch (start us, length us, event | category | flops | bytes accessed | tf_op | source)
XLA Modules:
  0.0 2049.3 jit_solution(15005382764682770103)
XLA Ops:
  7.2 0.0 all-gather.3.cloned.1.call-start
  7.2 31.0 %conditional.10 = (bf16[4096,1024]{1,0:T(8,128)(2,1)}) conditional(s32[]{:T(128)} %convert_element_type.36, f32[32768,128]{1,0:T(8,128)} %bitcast.184, f32[32768,128]{1,0:T(8,128)} %bitcast.185), branch_computations={%region_0.0_spmd, %region_1.0_spmd} | conditional | flops 4194304 | bytes 58720264 | solution.py:176
  7.2 8.9 convert_element_type.12
  16.1 12.5 convert_element_type.30
  28.6 9.6 copy.11
  38.3 0.3 reduce-scatter.11.cloned.1.call-start
  38.5 7.6 dynamic-slice_bitcast_fusion.x_ref.h_ref
  46.1 292.3 %all-gather.3.cloned.1.call-done.w_ref = bf16[32768,1024]{1,0:T(8,128)(2,1)} async-done(((bf16[4096,1024]{1,0:T(8,128)(2,1)}), bf16[32768,1024]{1,0:T(8,128)(2,1)}) %all-gather.3.cloned.1.call-update) | async-done | bytes 67108880 | tf_op jit(solution)/shard_map/all_gather | solution.py:181
  338.4 56.8 %up.4 = (bf16[4096,4096]{1,0:T(8,128)(2,1)}, bf16[4096,4096]{1,0:T(8,128)(2,1)}) custom-call(bf16[4096,1024]{1,0:T(8,128)(2,1)} %dynamic-slice_bitcast_fusion.x_ref.h_ref, bf16[32768,1024]{1,0:T(8,128)(2,1)} %all-gather.3.cloned.1.call-done.w_ref), custom_call_target="tpu_custom_call" | custom-call | flops 34359738368 | bytes 83886080 | tf_op jit(solution)/shard_map/up/pallas_call | solution.py:56
  395.3 42.1 %down.4.x_ref.h_ref = bf16[4096,1024]{1,0:T(8,128)(2,1)} custom-call(bf16[4096,4096]{1,0:T(8,128)(2,1)} %get-tuple-element.177.a_ref, bf16[32768,1024]{1,0:T(8,128)(2,1)} %all-gather.3.cloned.1.call-done.w_ref, bf16[4096,1024]{1,0:T(8,128)(2,1)} %dynamic-slice_bitcast_fusion.x_ref.h_ref), custom_call_target="tpu_custom_call" | custom-call | flops 34359738368 | bytes 83886080 | tf_op jit(solution)/shard_map/down/pallas_call | solution.py:76
  437.3 56.7 %up.5 = (bf16[4096,4096]{1,0:T(8,128)(2,1)}, bf16[4096,4096]{1,0:T(8,128)(2,1)}) custom-call(bf16[4096,1024]{1,0:T(8,128)(2,1)} %down.4.x_ref.h_ref, bf16[32768,1024]{1,0:T(8,128)(2,1)} %all-gather.3.cloned.1.call-done.w_ref), custom_call_target="tpu_custom_call" | custom-call | flops 34359738368 | bytes 83886080 | tf_op jit(solution)/shard_map/up/pallas_call | solution.py:56
  494.0 42.0 %down.5.x_ref.h_ref = bf16[4096,1024]{1,0:T(8,128)(2,1)} custom-call(bf16[4096,4096]{1,0:T(8,128)(2,1)} %get-tuple-element.178.a_ref, bf16[32768,1024]{1,0:T(8,128)(2,1)} %all-gather.3.cloned.1.call-done.w_ref, bf16[4096,1024]{1,0:T(8,128)(2,1)} %down.4.x_ref.h_ref), custom_call_target="tpu_custom_call" | custom-call | flops 34359738368 | bytes 83886080 | tf_op jit(solution)/shard_map/down/pallas_call | solution.py:76
  536.1 57.1 %up.6 = (bf16[4096,4096]{1,0:T(8,128)(2,1)}, bf16[4096,4096]{1,0:T(8,128)(2,1)}) custom-call(bf16[4096,1024]{1,0:T(8,128)(2,1)} %down.5.x_ref.h_ref, bf16[32768,1024]{1,0:T(8,128)(2,1)} %all-gather.3.cloned.1.call-done.w_ref), custom_call_target="tpu_custom_call" | custom-call | flops 34359738368 | bytes 83886080 | tf_op jit(solution)/shard_map/up/pallas_call | solution.py:56
  593.2 42.0 %down.6.x_ref.h_ref = bf16[4096,1024]{1,0:T(8,128)(2,1)} custom-call(bf16[4096,4096]{1,0:T(8,128)(2,1)} %get-tuple-element.179.a_ref, bf16[32768,1024]{1,0:T(8,128)(2,1)} %all-gather.3.cloned.1.call-done.w_ref, bf16[4096,1024]{1,0:T(8,128)(2,1)} %down.5.x_ref.h_ref), custom_call_target="tpu_custom_call" | custom-call | flops 34359738368 | bytes 83886080 | tf_op jit(solution)/shard_map/down/pallas_call | solution.py:76
  635.2 56.7 %up.7 = (bf16[4096,4096]{1,0:T(8,128)(2,1)}, bf16[4096,4096]{1,0:T(8,128)(2,1)}) custom-call(bf16[4096,1024]{1,0:T(8,128)(2,1)} %down.6.x_ref.h_ref, bf16[32768,1024]{1,0:T(8,128)(2,1)} %all-gather.3.cloned.1.call-done.w_ref), custom_call_target="tpu_custom_call" | custom-call | flops 34359738368 | bytes 83886080 | tf_op jit(solution)/shard_map/up/pallas_call | solution.py:56
  691.9 42.0 %down.7 = bf16[4096,1024]{1,0:T(8,128)(2,1)} custom-call(bf16[4096,4096]{1,0:T(8,128)(2,1)} %get-tuple-element.180.a_ref, bf16[32768,1024]{1,0:T(8,128)(2,1)} %all-gather.3.cloned.1.call-done.w_ref, bf16[4096,1024]{1,0:T(8,128)(2,1)} %down.6.x_ref.h_ref), custom_call_target="tpu_custom_call" | custom-call | flops 34359738368 | bytes 83886080 | tf_op jit(solution)/shard_map/down/pallas_call | solution.py:76
  734.0 11.9 multiply_convert_fusion
  745.8 62.5 %du.4.u_ref = bf16[4096,4096]{1,0:T(8,128)(2,1)} custom-call(bf16[4096,1024]{1,0:T(8,128)(2,1)} %get-tuple-element.195.g_ref, bf16[32768,1024]{1,0:T(8,128)(2,1)} %all-gather.3.cloned.1.call-done.w_ref, bf16[4096,4096]{1,0:T(8,128)(2,1)} %get-tuple-element.181.u_ref), custom_call_target="tpu_custom_call" | custom-call | flops 34359738368 | bytes 83886080 | tf_op jit(solution)/shard_map/du/pallas_call | solution.py:101
  808.4 44.0 %conditional.11 = (f32[4096,8,128]{2,1,0:T(8,128)}) conditional(s32[]{:T(128)} %convert_element_type.36, (bf16[4096,1024]{1,0:T(8,128)(2,1)}, bf16[4096,4096]{1,0:T(8,128)(2,1)}) %tuple.71, (bf16[4096,4096]{1,0:T(8,128)(2,1)}, bf16[4096,1024]{1,0:T(8,128)(2,1)}) %tuple.72), branch_computations={%region_2.3_spmd, %region_3.4_spmd} | conditional | flops 34359738368 | bytes 58720264 | solution.py:210
  808.4 43.6 %fusion.2 = f32[4096,1024]{1,0:T(8,128)} fusion(bf16[4096,4096]{1,0:T(8,128)(2,1)} %get-tuple-element.110, bf16[4096,1024]{1,0:T(8,128)(2,1)} %get-tuple-element.111), kind=kOutput, calls=%fused_computation.20 | convolution fusion | flops 34359738368 | bytes 58720256 | tf_op jit(solution)/shard_map/cond/branch_1_fun/dot_general | solution.py:32
  852.4 0.2 collective-permute-start
  852.6 42.3 %dx.3.g_ref = bf16[4096,1024]{1,0:T(8,128)(2,1)} custom-call(bf16[4096,4096]{1,0:T(8,128)(2,1)} %du.4.u_ref, bf16[32768,1024]{1,0:T(8,128)(2,1)} %all-gather.3.cloned.1.call-done.w_ref, bf16[4096,1024]{1,0:T(8,128)(2,1)} %get-tuple-element.195.g_ref), custom_call_target="tpu_custom_call" | custom-call | flops 34359738368 | bytes 83886080 | tf_op jit(solution)/shard_map/dx/pallas_call | solution.py:124
  895.0 43.0 %conditional.18 = (f32[4096,8,128]{2,1,0:T(8,128)}) conditional(s32[]{:T(128)} %convert_element_type.36, (bf16[4096,4096]{1,0:T(8,128)(2,1)}, bf16[4096,1024]{1,0:T(8,128)(2,1)}, f32[4096,8,128]{2,1,0:T(8,128)}) %tuple.88, (bf16[4096,1024]{1,0:T(8,128)(2,1)}, bf16[4096,4096]{1,0:T(8,128)(2,1)}, f32[4096,8,128]{2,1,0:T(8,128)}) %tuple.89), branch_computations={%region_22.23_spmd, %region_23.24_spmd} | conditional | flops 34363932672 | bytes 75497480 | solution.py:215
  895.0 43.0 %convolution_add_fusion.7 = f32[1024,4096]{1,0:T(8,128)} fusion(f32[1024,4096]{1,0:T(8,128)} %bitcast.70, bf16[4096,1024]{1,0:T(8,128)(2,1)} %get-tuple-element.151, bf16[4096,4096]{1,0:T(8,128)(2,1)} %get-tuple-element.152), kind=kOutput, calls=%fused_computation.7 | convolution fusion | flops 34363932672 | bytes 75497472 | tf_op jit(solution)/shard_map/cond/branch_1_fun/dot_general | solution.py:32
  938.0 0.2 reduce-scatter.9.cloned.1.call-start
  938.2 62.4 %du.5.u_ref = bf16[4096,4096]{1,0:T(8,128)(2,1)} custom-call(bf16[4096,1024]{1,0:T(8,128)(2,1)} %dx.3.g_ref, bf16[32768,1024]{1,0:T(8,128)(2,1)} %all-gather.3.cloned.1.call-done.w_ref, bf16[4096,4096]{1,0:T(8,128)(2,1)} %get-tuple-element.183.u_ref), custom_call_target="tpu_custom_call" | custom-call | flops 34359738368 | bytes 83886080 | tf_op jit(solution)/shard_map/du/pallas_call | solution.py:101
  1000.6 43.8 %conditional.12 = (f32[4096,8,128]{2,1,0:T(8,128)}) conditional(s32[]{:T(128)} %convert_element_type.36, (bf16[4096,1024]{1,0:T(8,128)(2,1)}, bf16[4096,4096]{1,0:T(8,128)(2,1)}) %tuple.74, (bf16[4096,4096]{1,0:T(8,128)(2,1)}, bf16[4096,1024]{1,0:T(8,128)(2,1)}) %tuple.75), branch_computations={%region_4.5_spmd, %region_5.6_spmd} | conditional | flops 34359738368 | bytes 58720264 | solution.py:210
  1000.8 43.6 %fusion.4 = f32[4096,1024]{1,0:T(8,128)} fusion(bf16[4096,4096]{1,0:T(8,128)(2,1)} %get-tuple-element.120, bf16[4096,1024]{1,0:T(8,128)(2,1)} %get-tuple-element.121), kind=kOutput, calls=%fused_computation.22 | convolution fusion | flops 34359738368 | bytes 58720256 | tf_op jit(solution)/shard_map/cond/branch_1_fun/dot_general | solution.py:32
  1044.4 0.1 collective-permute-start.1
  1044.5 42.3 %dx.4.g_ref = bf16[4096,1024]{1,0:T(8,128)(2,1)} custom-call(bf16[4096,4096]{1,0:T(8,128)(2,1)} %du.5.u_ref, bf16[32768,1024]{1,0:T(8,128)(2,1)} %all-gather.3.cloned.1.call-done.w_ref, bf16[4096,1024]{1,0:T(8,128)(2,1)} %dx.3.g_ref), custom_call_target="tpu_custom_call" | custom-call | flops 34359738368 | bytes 83886080 | tf_op jit(solution)/shard_map/dx/pallas_call | solution.py:124
  1086.8 43.4 %conditional.17 = (f32[4096,8,128]{2,1,0:T(8,128)}) conditional(s32[]{:T(128)} %convert_element_type.36, (bf16[4096,4096]{1,0:T(8,128)(2,1)}, bf16[4096,1024]{1,0:T(8,128)(2,1)}, f32[4096,8,128]{2,1,0:T(8,128)}) %tuple.86, (bf16[4096,1024]{1,0:T(8,128)(2,1)}, bf16[4096,4096]{1,0:T(8,128)(2,1)}, f32[4096,8,128]{2,1,0:T(8,128)}) %tuple.87), branch_computations={%region_18.19_spmd, %region_19.20_spmd} | conditional | flops 34363932672 | bytes 75497480 | solution.py:215
  1087.2 43.0 %convolution_add_fusion.5 = f32[1024,4096]{1,0:T(8,128)} fusion(f32[1024,4096]{1,0:T(8,128)} %bitcast.58, bf16[4096,1024]{1,0:T(8,128)(2,1)} %get-tuple-element.145, bf16[4096,4096]{1,0:T(8,128)(2,1)} %get-tuple-element.146), kind=kOutput, calls=%fused_computation.5 | convolution fusion | flops 34363932672 | bytes 75497472 | tf_op jit(solution)/shard_map/cond/branch_1_fun/dot_general | solution.py:32
  1130.3 0.0 reduce-scatter.7.cloned.1.call-start
  1130.3 62.3 %du.6.u_ref = bf16[4096,4096]{1,0:T(8,128)(2,1)} custom-call(bf16[4096,1024]{1,0:T(8,128)(2,1)} %dx.4.g_ref, bf16[32768,1024]{1,0:T(8,128)(2,1)} %all-gather.3.cloned.1.call-done.w_ref, bf16[4096,4096]{1,0:T(8,128)(2,1)} %get-tuple-element.185.u_ref), custom_call_target="tpu_custom_call" | custom-call | flops 34359738368 | bytes 83886080 | tf_op jit(solution)/shard_map/du/pallas_call | solution.py:101
  1192.7 52.0 %conditional.13 = (f32[4096,8,128]{2,1,0:T(8,128)}) conditional(s32[]{:T(128)} %convert_element_type.36, (bf16[4096,1024]{1,0:T(8,128)(2,1)}, bf16[4096,4096]{1,0:T(8,128)(2,1)}) %tuple.77, (bf16[4096,4096]{1,0:T(8,128)(2,1)}, bf16[4096,1024]{1,0:T(8,128)(2,1)}) %tuple.78), branch_computations={%region_6.7_spmd, %region_7.8_spmd} | conditional | flops 34359738368 | bytes 58720264 | solution.py:210
  1201.1 43.6 %fusion.6 = f32[4096,1024]{1,0:T(8,128)} fusion(bf16[4096,4096]{1,0:T(8,128)(2,1)} %get-tuple-element.124, bf16[4096,1024]{1,0:T(8,128)(2,1)} %get-tuple-element.125), kind=kOutput, calls=%fused_computation.24 | convolution fusion | flops 34359738368 | bytes 58720256 | tf_op jit(solution)/shard_map/cond/branch_1_fun/dot_general | solution.py:32
  1244.7 42.4 %dx.5.g_ref = bf16[4096,1024]{1,0:T(8,128)(2,1)} custom-call(bf16[4096,4096]{1,0:T(8,128)(2,1)} %du.6.u_ref, bf16[32768,1024]{1,0:T(8,128)(2,1)} %all-gather.3.cloned.1.call-done.w_ref, bf16[4096,1024]{1,0:T(8,128)(2,1)} %dx.4.g_ref), custom_call_target="tpu_custom_call" | custom-call | flops 34359738368 | bytes 83886080 | tf_op jit(solution)/shard_map/dx/pallas_call | solution.py:124
  1287.1 43.4 %conditional.16 = (f32[4096,8,128]{2,1,0:T(8,128)}) conditional(s32[]{:T(128)} %convert_element_type.36, (bf16[4096,4096]{1,0:T(8,128)(2,1)}, bf16[4096,1024]{1,0:T(8,128)(2,1)}, f32[4096,8,128]{2,1,0:T(8,128)}) %tuple.84, (bf16[4096,1024]{1,0:T(8,128)(2,1)}, bf16[4096,4096]{1,0:T(8,128)(2,1)}, f32[4096,8,128]{2,1,0:T(8,128)}) %tuple.85), branch_computations={%region_14.15_spmd, %region_15.16_spmd} | conditional | flops 34363932672 | bytes 75497480 | solution.py:215
  1287.5 43.0 %convolution_add_fusion.3 = f32[1024,4096]{1,0:T(8,128)} fusion(f32[1024,4096]{1,0:T(8,128)} %bitcast.46, bf16[4096,1024]{1,0:T(8,128)(2,1)} %get-tuple-element.139, bf16[4096,4096]{1,0:T(8,128)(2,1)} %get-tuple-element.140), kind=kOutput, calls=%fused_computation.3 | convolution fusion | flops 34363932672 | bytes 75497472 | tf_op jit(solution)/shard_map/cond/branch_1_fun/dot_general | solution.py:32
  1330.5 0.0 reduce-scatter.5.cloned.1.call-start
  1330.5 62.4 %du.7 = bf16[4096,4096]{1,0:T(8,128)(2,1)} custom-call(bf16[4096,1024]{1,0:T(8,128)(2,1)} %dx.5.g_ref, bf16[32768,1024]{1,0:T(8,128)(2,1)} %all-gather.3.cloned.1.call-done.w_ref, bf16[4096,4096]{1,0:T(8,128)(2,1)} %get-tuple-element.187.u_ref), custom_call_target="tpu_custom_call" | custom-call | flops 34359738368 | bytes 83886080 | tf_op jit(solution)/shard_map/du/pallas_call | solution.py:101
  1392.9 51.8 %conditional.14 = (f32[4096,8,128]{2,1,0:T(8,128)}) conditional(s32[]{:T(128)} %convert_element_type.36, (bf16[4096,1024]{1,0:T(8,128)(2,1)}, bf16[4096,4096]{1,0:T(8,128)(2,1)}) %tuple.80, (bf16[4096,4096]{1,0:T(8,128)(2,1)}, bf16[4096,1024]{1,0:T(8,128)(2,1)}) %tuple.81), branch_computations={%region_8.9_spmd, %region_9.10_spmd} | conditional | flops 34359738368 | bytes 58720264 | solution.py:210
  1401.1 43.6 %fusion.8 = f32[4096,1024]{1,0:T(8,128)} fusion(bf16[4096,4096]{1,0:T(8,128)(2,1)} %get-tuple-element.128, bf16[4096,1024]{1,0:T(8,128)(2,1)} %get-tuple-element.129), kind=kOutput, calls=%fused_computation.26 | convolution fusion | flops 34359738368 | bytes 58720256 | tf_op jit(solution)/shard_map/cond/branch_1_fun/dot_general | solution.py:32
  1444.7 25.2 %collective-permute-done.3 = f32[4096,8,128]{2,1,0:T(8,128)S(1)} collective-permute-done((f32[4096,8,128]{2,1,0:T(8,128)}, f32[4096,8,128]{2,1,0:T(8,128)S(1)}, u32[]{:S(2)}, u32[]{:S(2)}) %collective-permute-start.3) | collective-permute-done | bytes 16777248 | tf_op jit(solution)/shard_map/ppermute | solution.py:211
  1469.8 42.5 %conditional.15 = (f32[4096,8,128]{2,1,0:T(8,128)}) conditional(s32[]{:T(128)} %convert_element_type.36, (bf16[4096,4096]{1,0:T(8,128)(2,1)}, bf16[4096,1024]{1,0:T(8,128)(2,1)}, f32[4096,8,128]{2,1,0:T(8,128)S(1)}) %tuple.82, (bf16[4096,1024]{1,0:T(8,128)(2,1)}, bf16[4096,4096]{1,0:T(8,128)(2,1)}, f32[4096,8,128]{2,1,0:T(8,128)S(1)}) %tuple.83), branch_computations={%region_10.11_spmd, %region_11.12_spmd} | conditional | flops 34363932672 | bytes 75497480 | solution.py:215
  1470.1 42.3 %convolution_add_fusion.1 = f32[1024,4096]{1,0:T(8,128)} fusion(f32[1024,4096]{1,0:T(8,128)S(1)} %bitcast.205, bf16[4096,1024]{1,0:T(8,128)(2,1)} %get-tuple-element.133, bf16[4096,4096]{1,0:T(8,128)(2,1)} %get-tuple-element.134), kind=kOutput, calls=%fused_computation.1 | convolution fusion | flops 34363932672 | bytes 75497472 | tf_op jit(solution)/shard_map/cond/branch_1_fun/dot_general | solution.py:32
  1512.4 0.0 reduce-scatter.11.cloned.1.call-done
  1512.5 148.0 %reduce-scatter.5.cloned.1.call-done = f32[1024,8,128]{2,1,0:T(8,128)} async-done(((f32[4096,8,128]{2,1,0:T(8,128)}), f32[1024,8,128]{2,1,0:T(8,128)}) %reduce-scatter.5.cloned.1.call-update) | async-done | bytes 4194320 | tf_op jit(solution)/shard_map/reduce_scatter | solution.py:216
  1660.5 11.4 pad_maximum_fusion
  1671.9 7.0 all-to-all-start
  1678.9 0.0 all-gather.5.cloned.1.call-start
  1679.5 3.9 multiply_reduce_fusion.1
  1683.4 3.9 multiply_reduce_fusion.2
  1687.3 3.9 multiply_reduce_fusion.3
  1691.2 3.9 multiply_reduce_fusion.4
  1697.6 0.1 pad_maximum_fusion.1
  1698.3 180.5 %psum.7 = f32[2]{0:T(128)S(1)} all-reduce(f32[2]{0:T(128)S(1)} %pad_maximum_fusion.1), channel_id=1, replica_groups=mesh['stage'=4,'data'=2] {'stage','data'}, use_global_device_ids=true, to_apply=%region_27.28 | all-reduce | flops 2 | bytes 16 | tf_op jit(solution)/shard_map/psum | solution.py:218
  1878.8 0.6 fusion
  1880.2 14.5 conditional.19
  1880.2 14.2 copy.13
  1894.6 45.2 %adam.1 = (f32[32768,128]{1,0:T(8,128)}, f32[32768,128]{1,0:T(8,128)}, f32[32768,128]{1,0:T(8,128)}, bf16[32768,128]{1,0:T(8,128)(2,1)}) custom-call(f32[1]{0:T(128)} %bitcast.87.c_ref, f32[32768,128]{1,0:T(8,128)} %get-tuple-element.218.g_ref, f32[32768,128]{1,0:T(8,128)} %bitcast.186, f32[32768,128]{1,0:T(8,128)} %bitcast.190, f32[32768,128]{1,0:T(8,128)} %bitcast.191), custom_call_target="tpu_custom_call" | custom-call | tf_op jit(solution)/shard_map/adam/pallas_call | solution.py:154
  1939.9 14.0 reshape.200
  1954.6 48.4 %all-gather.5.cloned.1.call-done = bf16[1,1,8388608]{2,1,0:T(2,128)(2,1)} async-done(((bf16[1,1,4194304]{2,1,0:T(2,128)(2,1)}), bf16[1,1,8388608]{2,1,0:T(2,128)(2,1)}) %all-gather.5.cloned.1.call-update) | async-done | bytes 16777232 | tf_op jit(solution)/shard_map/all_gather | solution.py:228
  2003.0 37.8 %copy.36 = bf16[1,1,8388608]{2,1,0:T(2,128)(2,1)} copy(bf16[1,1,8388608]{2,1,0:T(2,128)(2,1)} %all-gather.5.cloned.1.call-done) | data formatting | bytes 33554432
  (14 shorter events, 0.1 us)
Async XLA Ops:
  7.2 331.3 %all-gather.3.cloned.1.call-start = ((), (), s32[]{:S(2)}) async-start(), calls=%async_computation.5 | async-start | bytes 75497472 | tf_op jit(solution)/shard_map/all_gather | solution.py:181
  38.3 1474.1 %reduce-scatter.11.cloned.1.call-start = ((), (), s32[]{:S(2)}) async-start(), calls=%async_computation.9 | async-start | bytes 20971520 | tf_op jit(solution)/shard_map/reduce_scatter | solution.py:216
  852.4 42.6 %collective-permute-start = (f32[4096,8,128]{2,1,0:T(8,128)}, f32[4096,8,128]{2,1,0:T(8,128)}, u32[]{:S(2)}, u32[]{:S(2)}) collective-permute-start(f32[4096,8,128]{2,1,0:T(8,128)} %get-tuple-element.210), channel_id=1, source_target_pairs={{0,1},{1,0},{2,3},{3,2},{4,5},{5,4},{6,7},{7,6}} | collective-permute-start | bytes 50331656 | tf_op jit(solution)/shard_map/ppermute | solution.py:211
  938.0 574.5 %reduce-scatter.9.cloned.1.call-start = ((), (), s32[]{:S(2)}) async-start(), calls=%async_computation.8 | async-start | bytes 20971520 | tf_op jit(solution)/shard_map/reduce_scatter | solution.py:216
  1044.4 42.4 %collective-permute-start.1 = (f32[4096,8,128]{2,1,0:T(8,128)}, f32[4096,8,128]{2,1,0:T(8,128)}, u32[]{:S(2)}, u32[]{:S(2)}) collective-permute-start(f32[4096,8,128]{2,1,0:T(8,128)} %get-tuple-element.211), channel_id=1, source_target_pairs={{0,1},{1,0},{2,3},{3,2},{4,5},{5,4},{6,7},{7,6}} | collective-permute-start | bytes 50331656 | tf_op jit(solution)/shard_map/ppermute | solution.py:211
  1130.3 382.2 %reduce-scatter.7.cloned.1.call-start = ((), (), s32[]{:S(2)}) async-start(), calls=%async_computation.7 | async-start | bytes 20971520 | tf_op jit(solution)/shard_map/reduce_scatter | solution.py:216
  1244.7 42.4 %collective-permute-start.2 = (f32[4096,8,128]{2,1,0:T(8,128)}, f32[4096,8,128]{2,1,0:T(8,128)}, u32[]{:S(2)}, u32[]{:S(2)}) collective-permute-start(f32[4096,8,128]{2,1,0:T(8,128)} %get-tuple-element.212), channel_id=1, source_target_pairs={{0,1},{1,0},{2,3},{3,2},{4,5},{5,4},{6,7},{7,6}} | collective-permute-start | bytes 50331656 | tf_op jit(solution)/shard_map/ppermute | solution.py:211
  1330.5 330.0 %reduce-scatter.5.cloned.1.call-start = ((), (), s32[]{:S(2)}) async-start(), calls=%async_computation.6 | async-start | bytes 20971520 | tf_op jit(solution)/shard_map/reduce_scatter | solution.py:216
  1444.7 25.2 %collective-permute-start.3 = (f32[4096,8,128]{2,1,0:T(8,128)}, f32[4096,8,128]{2,1,0:T(8,128)S(1)}, u32[]{:S(2)}, u32[]{:S(2)}) collective-permute-start(f32[4096,8,128]{2,1,0:T(8,128)} %get-tuple-element.213), channel_id=1, source_target_pairs={{0,1},{1,0},{2,3},{3,2},{4,5},{5,4},{6,7},{7,6}} | collective-permute-start | bytes 50331656 | tf_op jit(solution)/shard_map/ppermute | solution.py:211
  1671.9 208.3 %all-to-all-start = ((f32[4,1024,8,128]{3,2,1,0:T(8,128)}), f32[4,1024,8,128]{3,2,1,0:T(8,128)}, u32[]{:S(2)}, u32[]{:S(2)}) async-start(f32[4,1024,8,128]{3,2,1,0:T(8,128)} %pad_maximum_fusion), calls=%async_computation.4 | async-start | bytes 33554432 | tf_op jit(solution)/shard_map/all_to_all | solution.py:219
  1678.9 324.1 %all-gather.5.cloned.1.call-start = ((), (), s32[]{:S(2)}) async-start(), calls=%async_computation.10 | async-start | bytes 50331648 | tf_op jit(solution)/shard_map/all_gather | solution.py:228
Sparse Core Ops, SparseCore 0:
  38.4 300.0 all-gather.2
  938.1 147.9 reduce-scatter.10
  1130.4 147.9 reduce-scatter.8
  1330.6 147.9 reduce-scatter.6
  1512.5 147.9 reduce-scatter.4
  1954.1 48.9 all-gather.4
